TPU v7x, 8 devices: a whole 2x2x1 slice. The times are simulated.
8 devices in a mesh: data: 2 (over z, y), expert: 4 (over x, core).
Axes of the slice: x: 2, y: 2, z: 1, core: 2. Of those that a mesh axis runs over, the one named last changes fastest.
Arguments:
- tok_x: bfloat16 [12288, 768], P(('data', 'expert')), parts along dimension 0
- route_idx: int32 [12288, 1], P(('data', 'expert')), parts along dimension 0
- route_gate: float32 [12288, 1], P(('data', 'expert')), parts along dimension 0
- grad_y: bfloat16 [12288, 768], P(('data', 'expert')), parts along dimension 0
- w_gate: bfloat16 [256, 768, 256], P('expert')
- w_up: bfloat16 [256, 768, 256], P('expert')
- w_down: bfloat16 [256, 256, 768], P('expert')
Outputs:
- output 1: bfloat16 [12288, 768], P(('data', 'expert')), parts along dimension 0
- output 2: bfloat16 [12288, 768], P(('data', 'expert')), parts along dimension 0
- output 3: float32 [512, 768, 256], P(('data', 'expert')), parts along dimension 0
- output 4: float32 [512, 768, 256], P(('data', 'expert')), parts along dimension 0
- output 5: float32 [512, 256, 768], P(('data', 'expert')), parts along dimension 0
There are 2 independent parts. A program takes and returns all parts, laid end to end along the dimension named above; an argument that names none is the same for every part.
All inputs are finite; a program needn't handle non-finite values.
Results may differ from a plain program's by a relative error of at most 0.0094902.
Values are sent between devices in bfloat16 or wider.
A program may use at most 1 GiB of HBM per device.

v0:
```python
import jax
import jax.numpy as jnp
from jax import lax
from jax.sharding import PartitionSpec as P


def silu_parts(pre_act):
    sigmoid_a = jax.nn.sigmoid(pre_act)
    return pre_act * sigmoid_a, sigmoid_a * (1.0 + pre_act * (1.0 - sigmoid_a))


def route_tables(local_idx, num_experts, capacity):
    tok_count, top_count = local_idx.shape
    slot_count = tok_count * top_count
    hot_stride = num_experts // min(4, num_experts // 8)
    flat_ids = local_idx.reshape(slot_count)
    onehot = (flat_ids[:, None] == jnp.arange(num_experts, dtype=jnp.int32)[None, :]).astype(jnp.int32)
    position = jnp.sum(jnp.cumsum(onehot, axis=0) * onehot, axis=1) - 1
    is_kept = (flat_ids % hot_stride != 0) & (position < capacity)
    dest_row = jnp.where(is_kept, flat_ids * capacity + position, num_experts * capacity)
    slot_src = jnp.full((num_experts * capacity + 1,), slot_count, jnp.int32).at[dest_row].set(jnp.arange(slot_count, dtype=jnp.int32))
    return dest_row, slot_src[:num_experts * capacity]


def expert_forward(rows_x, w_in, w_lin, w_out, form_set):
    x_form, w_form, h_form, out_form, dw_form = form_set
    wo_form = w_form[:-2] + 'fd'
    pre_a = jnp.einsum(x_form + ',' + w_form + '->' + h_form, rows_x, w_in, preferred_element_type=jnp.float32).astype(jnp.bfloat16)
    pre_b = jnp.einsum(x_form + ',' + w_form + '->' + h_form, rows_x, w_lin, preferred_element_type=jnp.float32).astype(jnp.bfloat16)
    hidden = (jax.nn.silu(pre_a.astype(jnp.float32)) * pre_b.astype(jnp.float32)).astype(jnp.bfloat16)
    out_rows = jnp.einsum(h_form + ',' + wo_form + '->' + out_form, hidden, w_out, preferred_element_type=jnp.float32).astype(jnp.bfloat16)
    return (pre_a, pre_b, hidden), out_rows


def expert_backward(rows_x, grad_out, saved, w_in, w_lin, w_out, form_set):
    x_form, w_form, h_form, out_form, dw_form = form_set
    wo_form = w_form[:-2] + 'fd'
    dwo_form = dw_form[:-2] + 'fd'
    pre_a, pre_b, hidden = saved
    silu_a, silu_slope = silu_parts(pre_a.astype(jnp.float32))
    lin_b = pre_b.astype(jnp.float32)
    grad_h = jnp.einsum(out_form + ',' + wo_form + '->' + h_form, grad_out, w_out, preferred_element_type=jnp.float32).astype(jnp.bfloat16).astype(jnp.float32)
    grad_a = (grad_h * lin_b * silu_slope).astype(jnp.bfloat16)
    grad_b = (grad_h * silu_a).astype(jnp.bfloat16)
    back_form = h_form + ',' + w_form + '->' + out_form
    grad_in = (jnp.einsum(back_form, grad_a, w_in, preferred_element_type=jnp.float32) + jnp.einsum(back_form, grad_b, w_lin, preferred_element_type=jnp.float32)).astype(jnp.bfloat16)
    dw_spec = x_form + ',' + h_form + '->' + dw_form
    grad_w_in = jnp.einsum(dw_spec, rows_x, grad_a, preferred_element_type=jnp.float32)
    grad_w_lin = jnp.einsum(dw_spec, rows_x, grad_b, preferred_element_type=jnp.float32)
    grad_w_out = jnp.einsum(h_form + ',' + out_form + '->' + dwo_form, hidden, grad_out, preferred_element_type=jnp.float32)
    return grad_in, grad_w_in, grad_w_lin, grad_w_out


def solution(mesh):
    group_n = mesh.shape['expert']
    tok_spec = P(('data', 'expert'))
    weight_spec = P('expert')

    def shard_body(tok_x, route_idx, route_gate, grad_y, w_gate, w_up, w_down):
        tok_count, model_dim = tok_x.shape
        top_count = route_idx.shape[1]
        local_count = w_gate.shape[0]
        num_experts = local_count * group_n
        hot_count = min(4, num_experts // 8)
        hot_stride = num_experts // hot_count
        capacity = max(4, 2 * tok_count * top_count // num_experts)
        flat_rows = num_experts * capacity
        my_rank = lax.axis_index('expert')
        owner_list = [(slot_n * hot_stride) // local_count for slot_n in range(hot_count)]
        local_list = [(slot_n * hot_stride) % local_count for slot_n in range(hot_count)]

        def hot_copy(weights):
            picked = [jnp.where(my_rank == owner_n, weights[local_n], jnp.zeros_like(weights[local_n])) for owner_n, local_n in zip(owner_list, local_list)]
            return lax.psum(jnp.stack(picked), 'expert')

        hot_wg = hot_copy(w_gate)
        hot_wu = hot_copy(w_up)
        hot_wd = hot_copy(w_down)
        dest_row, slot_src = route_tables(route_idx, num_experts, capacity)
        tok_src = slot_src // top_count
        zero_row = jnp.zeros((1, model_dim), jnp.bfloat16)
        buf_shape = (group_n, local_count, capacity, model_dim)
        send_x = jnp.concatenate([tok_x, zero_row])[tok_src].reshape(buf_shape)
        recv_x = lax.all_to_all(send_x, 'expert', 0, 0)
        cold_forms = ('gecd', 'edf', 'gecf', 'gecd', 'edf')
        hot_forms = ('td', 'hdf', 'htf', 'htd', 'hdf')
        cold_saved, cold_out = expert_forward(recv_x, w_gate, w_up, w_down, cold_forms)
        back_out = lax.all_to_all(cold_out, 'expert', 0, 0)
        hot_saved, hot_out = expert_forward(tok_x, hot_wg, hot_wu, hot_wd, hot_forms)
        hot_ids = jnp.arange(hot_count, dtype=jnp.int32) * hot_stride
        hot_gate = jnp.sum(jnp.where(route_idx[None, :, :] == hot_ids[:, None, None], route_gate[None, :, :], 0.0), axis=2)
        out_slots = jnp.concatenate([back_out.reshape(flat_rows, model_dim), zero_row])[dest_row].reshape(tok_count, top_count, model_dim)
        out_y = jnp.sum(route_gate[:, :, None] * out_slots.astype(jnp.float32), axis=1) + jnp.sum(hot_gate[:, :, None] * hot_out.astype(jnp.float32), axis=0)
        gate_pad = jnp.concatenate([route_gate.reshape(tok_count * top_count), jnp.zeros((1,), jnp.float32)])
        send_gate = gate_pad[slot_src].reshape(group_n, local_count, capacity)
        send_dy = jnp.concatenate([grad_y, zero_row])[tok_src].reshape(buf_shape)
        recv_gate = lax.all_to_all(send_gate, 'expert', 0, 0)
        recv_dy = lax.all_to_all(send_dy, 'expert', 0, 0)
        cold_grad_out = (recv_gate[..., None] * recv_dy.astype(jnp.float32)).astype(jnp.bfloat16)
        cold_dx, cold_dwg, cold_dwu, cold_dwd = expert_backward(recv_x, cold_grad_out, cold_saved, w_gate, w_up, w_down, cold_forms)
        back_dx = lax.all_to_all(cold_dx, 'expert', 0, 0)
        hot_grad_out = (hot_gate[:, :, None] * grad_y.astype(jnp.float32)[None]).astype(jnp.bfloat16)
        hot_dx, hot_dwg, hot_dwu, hot_dwd = expert_backward(tok_x, hot_grad_out, hot_saved, hot_wg, hot_wu, hot_wd, hot_forms)
        dx_slots = jnp.concatenate([back_dx.reshape(flat_rows, model_dim), zero_row])[dest_row].reshape(tok_count, top_count, model_dim)
        grad_x = jnp.sum(dx_slots.astype(jnp.float32), axis=1) + jnp.sum(hot_dx.astype(jnp.float32), axis=0)
        hot_sums = lax.psum((hot_dwg, hot_dwu, hot_dwd), 'expert')
        grad_list = []
        for cold_w, hot_w in zip((cold_dwg, cold_dwu, cold_dwd), hot_sums):
            for slot_n in range(hot_count):
                cold_w = cold_w.at[local_list[slot_n]].add(jnp.where(my_rank == owner_list[slot_n], hot_w[slot_n], 0.0))
            grad_list.append(cold_w)
        return out_y.astype(jnp.bfloat16), grad_x.astype(jnp.bfloat16), grad_list[0], grad_list[1], grad_list[2]

    return jax.shard_map(shard_body, mesh=mesh, in_specs=(tok_spec, tok_spec, tok_spec, tok_spec, weight_spec, weight_spec, weight_spec), out_specs=(tok_spec, tok_spec, tok_spec, tok_spec, tok_spec), check_vma=False)
```

profile of v0, /device:TPU:0, one launch (start us, length us, event | category | flops | bytes accessed | tf_op | source)
XLA Modules:
  0.0 592.5 jit_solution(338343620634354426)
XLA Ops:
  13.5 1.3 pad_maximum_fusion.2
  14.8 1.3 pad_maximum_fusion.1
  16.2 1.4 pad_maximum_fusion
  19.9 6.2 %scatter_custom_fusion = s32[3073]{0:T(1024)S(1)} fusion(s32[1536]{0:T(1024)S(1)} %fusion.96, s32[1536]{0:T(1024)S(1)} %iota.16, s32[]{:T(128)} %constant.301.clone.1), kind=kCustom, calls=%fused_computation.147 | custom fusion | bytes 12296 | tf_op jit(solution)/shard_map/scatter | solution.py:21
  26.1 17.4 %gather_fusion.2 = f32[3072]{0:T(1024)S(1)} fusion(f32[1537]{0:T(1024)S(1)} %pad_maximum_fusion.3, s32[3072]{0:T(1024)S(1)} %fusion.93), kind=kCustom, calls=%fused_computation.2 | custom fusion | bytes 36864 | tf_op jit(solution)/shard_map/gather | solution.py:95
  44.5 4.6 all-to-all-start.2
  49.8 2.5 convert_element_type.168
  52.5 13.6 %gather_fusion.3 = bf16[3072,768]{1,0:T(8,128)(2,1)} fusion(bf16[1537,768]{1,0:T(8,128)(2,1)S(1)} %concatenate.42, s32[3072]{0:T(1024)S(1)} %fusion.93), kind=kCustom, calls=%fused_computation.3 | custom fusion | bytes 9449472 | tf_op jit(solution)/shard_map/gather | solution.py:96
  66.1 8.2 %reshape.474 = bf16[4,64,12,768]{3,2,1,0:T(8,128)(2,1)} reshape(bf16[3072,768]{1,0:T(8,128)(2,1)} %gather_fusion.3) | data formatting | bytes 9437184 | tf_op jit(solution)/shard_map/reshape | solution.py:96
  74.3 6.8 %copy.68 = bf16[4,64,12,768]{3,1,2,0:T(8,128)(2,1)} copy(bf16[4,64,12,768]{3,2,1,0:T(8,128)(2,1)} %reshape.474) | data formatting | bytes 9437184 | tf_op jit(solution)/shard_map/reshape | solution.py:96
  81.3 13.6 %gather_fusion = bf16[3072,768]{1,0:T(8,128)(2,1)} fusion(bf16[1537,768]{1,0:T(8,128)(2,1)S(1)} %concatenate.39, s32[3072]{0:T(1024)S(1)} %fusion.93), kind=kCustom, calls=%fused_computation | custom fusion | bytes 9449472 | tf_op jit(solution)/shard_map/gather | solution.py:83
  94.9 8.2 %reshape.471 = bf16[4,64,12,768]{3,2,1,0:T(8,128)(2,1)} reshape(bf16[3072,768]{1,0:T(8,128)(2,1)} %gather_fusion) | data formatting | bytes 9437184 | tf_op jit(solution)/shard_map/reshape | solution.py:83
  103.1 6.6 %copy.59 = bf16[4,64,12,768]{3,1,2,0:T(8,128)(2,1)} copy(bf16[4,64,12,768]{3,2,1,0:T(8,128)(2,1)} %reshape.471) | data formatting | bytes 9437184 | tf_op jit(solution)/shard_map/reshape | solution.py:83
  109.7 5.1 all-to-all-start.3
  116.6 4.4 convolution_convert_fusion
  121.1 2.9 convolution_convert_fusion.1
  124.0 5.2 fusion.12
  129.3 5.6 fusion.25
  135.0 5.5 fusion.59
  140.5 4.3 fusion.56
  144.8 9.9 %fusion.116 = f32[4,1536,768]{2,1,0:T(8,128)} fusion(bf16[4,1536,256]{1,2,0:T(8,128)(2,1)S(1)} %get-tuple-element.179, bf16[4,768,256]{1,2,0:T(8,128)(2,1)} %get-tuple-element.154), kind=kOutput, calls=%fused_computation.163 | convolution fusion | flops 2415919104 | bytes 23592960 | tf_op jit(solution)/shard_map/htf,hdf->htd/dot_general | solution.py:46
  154.7 13.0 %convert_reduce_fusion = f32[1536,768]{1,0:T(8,128)} fusion(f32[4,1536,768]{2,1,0:T(8,128)} %fusion.116, bf16[4,768,256]{1,2,0:T(8,128)(2,1)S(1)} %copy-done.22, bf16[4,1536,256]{1,2,0:T(8,128)(2,1)} %copy-done.26, bf16[4,256,1536]{2,1,0:T(8,128)(2,1)S(1)} %copy-done.25), kind=kOutput, calls=%fused_computation.18 | convolution fusion | flops 2446196736 | bytes 31457280 | tf_op jit(solution)/shard_map/htf,hdf->htd/dot_general | solution.py:46
  167.7 17.8 %all-to-all-done.3 = bf16[4,64,12,768]{3,1,2,0:T(8,128)(2,1)} async-done(((bf16[4,64,12,768]{3,1,2,0:T(8,128)(2,1)}), bf16[4,64,12,768]{3,1,2,0:T(8,128)(2,1)}, u32[]{:S(2)}, u32[]{:S(2)}) %all-to-all-start.3) | async-done | bytes 4718624 | tf_op jit(solution)/shard_map/all_to_all | solution.py:98
  185.5 5.1 all-to-all-start
  190.7 8.8 %multiply_reduce_fusion = f32[1536,768]{1,0:T(8,128)} fusion(f32[4,1536]{1,0:T(4,128)S(1)} %compare_select_fusion.4, bf16[4,256,768]{2,1,0:T(8,128)(2,1)S(1)} %copy-done.21, bf16[4,256,1536]{2,1,0:T(8,128)(2,1)} %copy-done.23, bf16[4,256,1536]{2,1,0:T(8,128)(2,1)} %copy-done.24), kind=kOutput, calls=%fused_computation.21 | convolution fusion | flops 2446196736 | bytes 12607488 | tf_op jit(solution)/shard_map/htf,hfd->htd/dot_general | solution.py:31
  199.5 5.3 multiply_convert_fusion.3
  204.8 14.4 %fusion.62 = bf16[64,4,12,256]{3,2,1,0:T(8,128)(2,1)} fusion(bf16[64,256,768]{2,1,0:T(8,128)(2,1)} %param.37, bf16[4,64,12,768]{3,1,2,0:T(8,128)(2,1)} %multiply_convert_fusion.3), kind=kOutput, calls=%fused_computation.87 | convolution fusion | flops 1208745984 | bytes 31457280 | tf_op jit(solution)/shard_map/gecd,efd->gecf/dot_general | solution.py:42
  219.3 75.4 %all-to-all-done = bf16[4,64,12,768]{3,1,2,0:T(8,128)(2,1)} async-done(((bf16[4,64,12,768]{3,1,2,0:T(8,128)(2,1)}), bf16[4,64,12,768]{3,1,2,0:T(8,128)(2,1)}, u32[]{:S(2)}, u32[]{:S(2)}) %all-to-all-start) | async-done | bytes 4718624 | tf_op jit(solution)/shard_map/all_to_all | solution.py:84
  294.7 14.1 %fusion.67 = bf16[64,4,12,256]{3,2,1,0:T(8,128)(2,1)S(1)} fusion(bf16[64,768,256]{2,1,0:T(8,128)(2,1)} %param.35, bf16[4,64,12,768]{3,1,2,0:T(8,128)(2,1)} %all-to-all-done), kind=kOutput, calls=%fused_computation.88 | convolution fusion | flops 1208745984 | bytes 31457280 | tf_op jit(solution)/shard_map/gecd,edf->gecf/dot_general | solution.py:28
  308.8 18.1 %fusion = f32[64,4,12,768]{3,2,1,0:T(8,128)} fusion(bf16[64,768,256]{2,1,0:T(8,128)(2,1)} %param.36, bf16[64,4,12,256]{3,2,1,0:T(8,128)(2,1)} %fusion.62, bf16[64,4,12,256]{3,2,1,0:T(8,128)(2,1)S(1)} %fusion.67), kind=kOutput, calls=%fused_computation.6 | convolution fusion | flops 1214251008 | bytes 37748736 | tf_op jit(solution)/shard_map/gecf,edf->gecd/dot_general | solution.py:46
  327.0 15.4 %fusion.72 = bf16[64,4,12,256]{3,2,1,0:T(8,128)(2,1)} fusion(bf16[64,768,256]{2,1,0:T(8,128)(2,1)} %param.36, bf16[4,64,12,768]{3,1,2,0:T(8,128)(2,1)} %all-to-all-done), kind=kOutput, calls=%fused_computation.89 | convolution fusion | flops 1208745984 | bytes 31457280 | tf_op jit(solution)/shard_map/gecd,edf->gecf/dot_general | solution.py:29
  342.4 18.8 %fusion.27 = bf16[4,64,12,768]{3,2,0,1:T(8,128)(2,1)} fusion(f32[64,4,12,768]{3,2,1,0:T(8,128)} %fusion, bf16[64,768,256]{2,1,0:T(8,128)(2,1)} %param.35, bf16[64,4,12,256]{3,2,1,0:T(8,128)(2,1)} %fusion.62, bf16[64,4,12,256]{3,2,1,0:T(8,128)(2,1)} %fusion.72, bf16[64,4,12,256]{3,2,1,0:T(8,128)(2,1)S(1)} %fusion.67), kind=kOutput, calls=%fused_computation.44 | convolution fusion | flops 1222901760 | bytes 44040192 | tf_op jit(solution)/shard_map/gecf,edf->gecd/dot_general | solution.py:46
  361.3 7.5 %copy.70 = bf16[4,64,12,768]{3,1,2,0:T(8,128)(2,1)} copy(bf16[4,64,12,768]{3,2,0,1:T(8,128)(2,1)} %fusion.27) | data formatting | bytes 9437184 | tf_op jit(solution)/shard_map/convert_element_type | solution.py:46
  368.8 5.1 all-to-all-start.4
  373.9 15.7 %convert_bitcast_fusion = bf16[4,64,12,768]{3,2,0,1:T(8,128)(2,1)} fusion(bf16[64,256,768]{2,1,0:T(8,128)(2,1)} %param.37, bf16[64,4,12,256]{3,2,1,0:T(8,128)(2,1)} %fusion.72, bf16[64,4,12,256]{3,2,1,0:T(8,128)(2,1)S(1)} %fusion.67), kind=kOutput, calls=%fused_computation.55 | convolution fusion | flops 1216610304 | bytes 33030144 | tf_op jit(solution)/shard_map/gecf,efd->gecd/dot_general | solution.py:31
  389.6 7.7 %copy.62 = bf16[4,64,12,768]{3,1,2,0:T(8,128)(2,1)} copy(bf16[4,64,12,768]{3,2,0,1:T(8,128)(2,1)} %convert_bitcast_fusion) | data formatting | bytes 9437184 | tf_op jit(solution)/shard_map/convert_element_type | solution.py:31
  397.2 22.3 %convolution_bitcast_fusion.2 = f32[64,768,256]{2,1,0:T(8,128)} fusion(bf16[4,64,12,768]{3,1,2,0:T(8,128)(2,1)} %all-to-all-done, bf16[64,4,12,256]{3,2,1,0:T(8,128)(2,1)S(1)} %copy-done, bf16[64,4,12,256]{3,2,1,0:T(8,128)(2,1)} %fusion.72, bf16[64,4,12,256]{3,2,1,0:T(8,128)(2,1)S(1)} %fusion.67), kind=kOutput, calls=%fused_computation.24 | convolution fusion | flops 1218183168 | bytes 59768832 | tf_op jit(solution)/shard_map/gecd,gecf->edf/dot_general | solution.py:48
  419.5 9.2 %all-to-all-done.4 = bf16[4,64,12,768]{3,1,2,0:T(8,128)(2,1)} async-done(((bf16[4,64,12,768]{3,1,2,0:T(8,128)(2,1)}), bf16[4,64,12,768]{3,1,2,0:T(8,128)(2,1)}, u32[]{:S(2)}, u32[]{:S(2)}) %all-to-all-start.4) | async-done | bytes 4718624 | tf_op jit(solution)/shard_map/all_to_all | solution.py:101
  428.7 5.2 all-to-all-start.1
  433.9 21.6 %convolution_bitcast_fusion.1 = f32[64,768,256]{2,1,0:T(8,128)} fusion(bf16[4,64,12,768]{3,1,2,0:T(8,128)(2,1)} %all-to-all-done, bf16[64,4,12,256]{3,2,1,0:T(8,128)(2,1)} %fusion.62, bf16[64,4,12,256]{3,2,1,0:T(8,128)(2,1)S(1)} %fusion.67), kind=kOutput, calls=%fused_computation.23 | convolution fusion | flops 1214251008 | bytes 58195968 | tf_op jit(solution)/shard_map/gecd,gecf->edf/dot_general | solution.py:49
  455.5 1.2 slice.348
  456.7 1.2 copy.105
  460.2 21.7 %convolution_bitcast_fusion = f32[64,256,768]{2,1,0:T(8,128)} fusion(bf16[4,64,12,768]{3,1,2,0:T(8,128)(2,1)} %multiply_convert_fusion.3, bf16[64,4,12,256]{3,2,1,0:T(8,128)(2,1)} %fusion.72, bf16[64,4,12,256]{3,2,1,0:T(8,128)(2,1)S(1)} %fusion.67), kind=kOutput, calls=%fused_computation.22 | convolution fusion | flops 1214251008 | bytes 58195968 | tf_op jit(solution)/shard_map/gecf,gecd->efd/dot_general | solution.py:50
  481.9 7.8 %copy.71 = bf16[4,64,12,768]{3,2,1,0:T(8,128)(2,1)} copy(bf16[4,64,12,768]{3,1,2,0:T(8,128)(2,1)} %all-to-all-done.4) | data formatting | bytes 9437184 | tf_op jit(solution)/shard_map/all_to_all | solution.py:101
  489.8 8.6 %reshape.475 = bf16[3072,768]{1,0:T(8,128)(2,1)} reshape(bf16[4,64,12,768]{3,2,1,0:T(8,128)(2,1)} %copy.71) | data formatting | bytes 9437184 | tf_op jit(solution)/shard_map/reshape | solution.py:104
  498.3 4.8 concatenate.43
  503.1 7.8 %copy.63 = bf16[4,64,12,768]{3,2,1,0:T(8,128)(2,1)} copy(bf16[4,64,12,768]{3,1,2,0:T(8,128)(2,1)} %all-to-all-done.1) | data formatting | bytes 9437184 | tf_op jit(solution)/shard_map/all_to_all | solution.py:88
  511.0 8.4 %reshape.472 = bf16[3072,768]{1,0:T(8,128)(2,1)} reshape(bf16[4,64,12,768]{3,2,1,0:T(8,128)(2,1)} %copy.63) | data formatting | bytes 9437184 | tf_op jit(solution)/shard_map/reshape | solution.py:92
  519.4 4.7 concatenate.40
  524.1 9.0 %gather_fusion.4 = bf16[1536,768]{1,0:T(8,128)(2,1)S(1)} fusion(bf16[3073,768]{1,0:T(8,128)(2,1)} %concatenate.43, s32[2048]{0:T(1024)S(1)} %copy-done.17), kind=kCustom, calls=%fused_computation.4 | custom fusion | bytes 4724736 | tf_op jit(solution)/shard_map/gather | solution.py:104
  533.2 9.7 %gather_fusion.1 = bf16[1536,768]{1,0:T(8,128)(2,1)} fusion(bf16[3073,768]{1,0:T(8,128)(2,1)} %concatenate.40, s32[2048]{0:T(1024)S(1)} %copy-done.17), kind=kCustom, calls=%fused_computation.1 | custom fusion | bytes 4724736 | tf_op jit(solution)/shard_map/gather | solution.py:92
  542.9 5.9 fusion.84
  548.8 1.4 copy.79
  551.1 2.3 copy.80
  553.5 2.3 copy.81
  555.8 1.4 copy.82
  557.2 2.3 copy.85
  559.4 2.1 constant_dynamic-update-slice_fusion.5
  561.5 2.3 copy.86
  563.8 2.3 copy.87
  566.1 2.3 copy.88
  568.4 2.5 constant_dynamic-update-slice_fusion.1
  570.9 2.3 fusion.92
  580.8 4.5 add_convert_fusion.2
  (116 shorter events, 23.2 us)
Async XLA Ops:
  7.2 4.3 slice-start
  7.2 109.4 %all-reduce.11.cloned.1.call-start = ((), (), s32[]{:S(2)}) async-start(), calls=%async_computation.6 | async-start | bytes 9437184 | tf_op jit(solution)/shard_map/psum | solution.py:74
  16.1 1.4 copy-start.18
  18.1 1.2 copy-start.19
  19.3 29.8 %copy-start.15 = (f32[1536]{0:T(1024)}, f32[1536]{0:T(1024)S(1)}, u32[]{:S(2)}) copy-start(f32[1536]{0:T(1024)S(1)} %reduce.24) | copy-start | bytes 18436
  26.1 23.7 %copy-start.2 = (bf16[1536,768]{1,0:T(8,128)(2,1)S(1)}, bf16[1536,768]{1,0:T(8,128)(2,1)}, u32[]{:S(2)}) copy-start(bf16[1536,768]{1,0:T(8,128)(2,1)} %param.34) | copy-start | bytes 7077892
  44.5 65.2 %all-to-all-start.2 = ((f32[4,1,768]{2,1,0:T(1,128)}), f32[4,1,768]{2,1,0:T(1,128)S(1)}, u32[]{:S(2)}, u32[]{:S(2)}) async-start(f32[4,1,768]{2,1,0:T(1,128)} %reshape.540), calls=%async_computation.2 | async-start | bytes 24576 | tf_op jit(solution)/shard_map/all_to_all | solution.py:97
  49.1 3.2 copy-start.3
  74.3 6.8 %copy-start.12 = (bf16[1536,768]{1,0:T(8,128)(2,1)S(1)}, bf16[1536,768]{1,0:T(8,128)(2,1)}, u32[]{:S(2)}) copy-start(bf16[1536,768]{1,0:T(8,128)(2,1)} %param.31) | copy-start | bytes 7077892
  109.7 6.9 %copy-start.13 = (bf16[1536,768]{1,0:T(8,128)(2,1)S(1)}, bf16[1536,768]{1,0:T(8,128)(2,1)}, u32[]{:S(2)}) copy-start(bf16[1536,768]{1,0:T(8,128)(2,1)} %param.31) | copy-start | bytes 7077892
  109.7 75.8 %all-to-all-start.3 = ((bf16[4,64,12,768]{3,1,2,0:T(8,128)(2,1)}), bf16[4,64,12,768]{3,1,2,0:T(8,128)(2,1)}, u32[]{:S(2)}, u32[]{:S(2)}) async-start(bf16[4,64,12,768]{3,1,2,0:T(8,128)(2,1)} %copy.68), calls=%async_computation.3 | async-start | bytes 9437184 | tf_op jit(solution)/shard_map/all_to_all | solution.py:98
  114.8 428.1 %all-reduce.9.cloned.1.call-start = ((), (), s32[]{:S(2)}) async-start(), calls=%async_computation.5 | async-start | bytes 18874368 | tf_op jit(solution)/shard_map/psum | solution.py:106
  116.6 4.5 copy-start.5
  116.6 7.4 %slice-start.1 = ((s8[4718592]{0:T(1024)(128)(4,1)}), s8[4194304]{0:T(1024)(128)(4,1)S(1)}, s32[]{:S(2)}) async-start(s8[4718592]{0:T(1024)(128)(4,1)} %bitcast.168), calls=%async_computation.8 | async-start | bytes 8388608
  121.1 8.2 %copy-start.23 = (bf16[4,256,1536]{2,1,0:T(8,128)(2,1)}, bf16[4,256,1536]{2,1,0:T(8,128)(2,1)S(1)}, u32[]{:S(2)}) copy-start(bf16[4,256,1536]{2,1,0:T(8,128)(2,1)S(1)} %convolution_convert_fusion) | copy-start | bytes 9437188
  121.1 2.9 slice-start.2
  124.0 10.9 %copy-start.24 = (bf16[4,256,1536]{2,1,0:T(8,128)(2,1)}, bf16[4,256,1536]{2,1,0:T(8,128)(2,1)S(1)}, u32[]{:S(2)}) copy-start(bf16[4,256,1536]{2,1,0:T(8,128)(2,1)S(1)} %convolution_convert_fusion.1) | copy-start | bytes 9437188
  124.0 5.3 copy-start.20
  129.3 5.6 copy-start.14
  134.9 5.5 copy-start.26
  144.8 9.9 %copy-start.22 = (bf16[4,768,256]{1,2,0:T(8,128)(2,1)S(1)}, bf16[4,768,256]{1,2,0:T(8,128)(2,1)}, u32[]{:S(2)}) copy-start(bf16[4,768,256]{1,2,0:T(8,128)(2,1)} %get-tuple-element.153) | copy-start | bytes 4718596
  144.8 9.9 %copy-start.25 = (bf16[4,256,1536]{2,1,0:T(8,128)(2,1)S(1)}, bf16[4,256,1536]{2,1,0:T(8,128)(2,1)}, u32[]{:S(2)}) copy-start(bf16[4,256,1536]{2,1,0:T(8,128)(2,1)} %copy-done.24) | copy-start | bytes 9437188
  167.7 22.9 %copy-start.21 = (bf16[4,256,768]{2,1,0:T(8,128)(2,1)S(1)}, bf16[4,256,768]{2,1,0:T(8,128)(2,1)}, u32[]{:S(2)}) copy-start(bf16[4,256,768]{2,1,0:T(8,128)(2,1)} %get-tuple-element.152) | copy-start | bytes 4718596
  185.5 109.2 %all-to-all-start = ((bf16[4,64,12,768]{3,1,2,0:T(8,128)(2,1)}), bf16[4,64,12,768]{3,1,2,0:T(8,128)(2,1)}, u32[]{:S(2)}, u32[]{:S(2)}) async-start(bf16[4,64,12,768]{3,1,2,0:T(8,128)(2,1)} %copy.59), calls=%async_computation | async-start | bytes 9437184 | tf_op jit(solution)/shard_map/all_to_all | solution.py:84
  368.8 59.9 %all-to-all-start.4 = ((bf16[4,64,12,768]{3,1,2,0:T(8,128)(2,1)}), bf16[4,64,12,768]{3,1,2,0:T(8,128)(2,1)}, u32[]{:S(2)}, u32[]{:S(2)}) async-start(bf16[4,64,12,768]{3,1,2,0:T(8,128)(2,1)} %copy.70), calls=%async_computation.4 | async-start | bytes 9437184 | tf_op jit(solution)/shard_map/all_to_all | solution.py:101
  389.6 7.7 %copy-start = (bf16[64,4,12,256]{3,2,1,0:T(8,128)(2,1)S(1)}, bf16[64,4,12,256]{3,2,1,0:T(8,128)(2,1)}, u32[]{:S(2)}) copy-start(bf16[64,4,12,256]{3,2,1,0:T(8,128)(2,1)} %fusion.62) | copy-start | bytes 4718596
  428.7 74.5 %all-to-all-start.1 = ((bf16[4,64,12,768]{3,1,2,0:T(8,128)(2,1)}), bf16[4,64,12,768]{3,1,2,0:T(8,128)(2,1)}, u32[]{:S(2)}, u32[]{:S(2)}) async-start(bf16[4,64,12,768]{3,1,2,0:T(8,128)(2,1)} %copy.62), calls=%async_computation.1 | async-start | bytes 9437184 | tf_op jit(solution)/shard_map/all_to_all | solution.py:88
  519.4 4.7 copy-start.17
  533.2 9.7 %copy-start.11 = (f32[1,768,256]{1,2,0:T(8,128)S(1)}, f32[1,768,256]{1,2,0:T(8,128)}, u32[]{:S(2)}) copy-start(f32[1,768,256]{1,2,0:T(8,128)} %copy.105) | copy-start | bytes 2359300
  568.4 4.8 copy-start.4
  568.4 5.8 copy-start.6
  570.9 4.2 copy-start.7
  570.9 9.9 %slice-start.3 = ((s8[4718592]{0:T(1024)(128)(4,1)}), s8[4194304]{0:T(1024)(128)(4,1)S(1)}, s32[]{:S(2)}) async-start(s8[4718592]{0:T(1024)(128)(4,1)} %bitcast.170), calls=%async_computation.10 | async-start | bytes 8388608
  573.2 3.8 copy-start.8
  573.2 4.8 copy-start.9
  574.2 4.7 copy-start.10
  575.1 5.6 slice-start.4
  576.1 4.7 copy-start.1
  576.1 4.7 copy-start.16
Sparse Core Ops, SparseCore 0:
  17.7 91.2 all-reduce.10
  144.9 235.2 all-reduce.8
where the time goes:
time: 602 us; the launch traced here: 593 us
  matrix products  222 us (37%)
  local copies, waits for them, and re-layouts  193 us (32%)
  waiting for transfers between devices  102 us (17%)
  other arithmetic  34.9 us (6%)
  starting transfers between devices  25.6 us (4%)
  between operations  15 us (2%)
    all_to_all x1, waiting for transfers between devices, shard_body(): recv_x = lax.all_to_all(send_x, 'expert', 0, 0)  75.4 us
    dot_general x2, matrix products, expert_backward(): jnp.einsum(back_form, grad_b, w_lin, preferred_element_type=jnp.float32)  31.2 us
    dot_general x2, matrix products, expert_backward(): jnp.einsum(back_form, grad_a, w_in, preferred_element_type=jnp.float32)  28.7 us
    dot_general x2, matrix products, expert_backward(): jnp.einsum(dw_spec, rows_x, grad_b, preferred_element_type=jnp.float32)  27.1 us
    dot_general x2, matrix products, expert_backward(): jnp.einsum(h_form + ',' + out_form + '->' + dwo_form, hidden, grad_out, p...  26.9 us
    dot_general x2, matrix products, expert_backward(): jnp.einsum(dw_spec, rows_x, grad_a, preferred_element_type=jnp.float32)  26.6 us
    dot_general x2, matrix products, expert_forward(): jnp.einsum(h_form + ',' + wo_form + '->' + out_form, hidden, w_out, prefe...  24.5 us
    dot_general x2, matrix products, expert_backward(): jnp.einsum(out_form + ',' + wo_form + '->' + h_form, grad_out, w_out, pre...  20 us
  transfers between devices with their start and end apart: 7, of which 3 were waited for; matrix products, arithmetic and copies ran while one was open for 67% of the time, Pallas kernels for 0%

commit v1 on v0

v1 whole, which is shorter than its diff:
```python
import functools

import jax
import jax.numpy as jnp
from jax import lax
from jax.experimental import pallas as pl
from jax.experimental.pallas import tpu as pltpu
from jax.sharding import PartitionSpec as P

BF16, F32, I32 = jnp.bfloat16, jnp.float32, jnp.int32
WIN = 32
LIST = 4096
COL_ROUNDS, COL_HI, COL_LO = 66, 128, 192


def iota(shape, dim):
    return lax.broadcasted_iota(I32, shape, dim)


def exact_dot(lhs, rhs):
    return jnp.dot(lhs, rhs, precision=lax.Precision.HIGHEST, preferred_element_type=F32)


def mm(lhs, rhs):
    return jnp.dot(lhs, rhs, preferred_element_type=F32)


def mm_nt(lhs, rhs):
    return lax.dot_general(lhs, rhs, (((1,), (1,)), ((), ())), preferred_element_type=F32)


def mm_tn(lhs, rhs):
    return lax.dot_general(lhs, rhs, (((0,), (0,)), ((), ())), preferred_element_type=F32)


def to_column(row):
    wide = jnp.broadcast_to(row, (128, row.shape[1]))
    return jnp.transpose(wide)[:, :1]


def route_kernel(capacity, caps, ids_ref, vslot_ref, tbl_ref, pos_ref):
    blocks = ids_ref.shape[1] // 256
    er = iota((256, 256), 0)
    ec = iota((256, 256), 1)
    upper = jnp.where(er < ec, 1.0, 0.0).astype(BF16)
    carry = jnp.zeros((256, 1), F32)
    for b in range(blocks):
        span = slice(b * 256, (b + 1) * 256)
        oh = jnp.where(er == ids_ref[:, span], 1.0, 0.0)
        cum = mm(oh.astype(BF16), upper) + carry
        pos_ref[:, span] = jnp.sum(oh * cum, axis=0, keepdims=True)
        carry = carry + jnp.sum(oh, axis=1, keepdims=True)
    hot = (er[:, :1] & 63) == 0
    cnt = jnp.where(hot, carry, jnp.minimum(carry, float(capacity)))
    cold_cnt = jnp.broadcast_to(jnp.where(hot, 0.0, cnt), (256, 128))
    dr, dc = er >> 6, ec >> 6
    same = jnp.where(dr == dc, 1.0, 0.0)
    cold_tot = exact_dot(same, cold_cnt)[:, :1]
    rel = exact_dot(jnp.where(ec < er, same, 0.0), cold_cnt)[:, :1]
    rounds = jnp.ones((256, 1), F32)
    for k in range(1, 1 + ids_ref.shape[1] // min(caps)):
        more = (cold_tot > float(k * caps[0])) | (hot & (cnt > float(k * caps[1])))
        rounds = rounds + jnp.where(more, 1.0, 0.0)
    rounds = jnp.max(rounds, axis=0, keepdims=True)
    lm = er & 63
    rel_hi = jnp.floor(rel * 0.0625)
    table = jnp.where((ec == lm) & (lm > 0), cnt, 0.0)
    table += jnp.where(ec == lm + COL_HI, rel_hi, 0.0) + jnp.where(ec == lm + COL_LO, rel - 16.0 * rel_hi, 0.0)
    table += jnp.where((ec == COL_ROUNDS) & (lm == 0), rounds, 0.0)
    pick = jnp.where((iota((8, 256), 1) >> 6) == iota((8, 256), 0), 1.0, 0.0)
    tbl_ref[...] = exact_dot(pick, table)
    start = (dr[:, :1] * LIST).astype(F32) + jnp.where(hot, float(4 * LIST), rel)
    for b in range(blocks):
        span = slice(b * 256, (b + 1) * 256)
        ids = ids_ref[:, span]
        pos = pos_ref[:, span]
        mine = jnp.sum(jnp.where(er == ids, start, 0.0), axis=0, keepdims=True)
        kept = ((ids & 63) == 0) | (pos < float(capacity))
        vslot_ref[:, span] = jnp.where(kept, mine + pos, -1.0).astype(I32)


def pack_kernel(first_list, cap, round_ref, vslot_ref, gate_ref, x_ref, dy_ref, tbl_ref, send_ref, g_ref):
    step = pl.program_id(0)
    tok_n, d = x_ref.shape
    rows_n = send_ref.shape[0]

    @pl.when(step == 0)
    def _():
        for b in range(tok_n // 256):
            span = slice(b * 256, (b + 1) * 256)
            gate = to_column(gate_ref[:, span])
            g_ref[span, :] = (gate * dy_ref[span, :].astype(F32)).astype(BF16)

    row = iota((rows_n, tok_n), 0)
    want = row + (first_list + step) * LIST + round_ref[0] * cap
    if cap < rows_n:
        want = jnp.where(row < cap, want, -2)
    perm = jnp.where(want == vslot_ref[...], 1.0, 0.0).astype(BF16)
    x = mm(perm, x_ref[...])
    if cap < rows_n:
        tbl = tbl_ref[pl.ds(step, 1), :]
        tbl = jnp.concatenate([tbl, jnp.zeros((1, d - tbl.shape[1]), F32)], axis=1)
        x = jnp.where(iota(x.shape, 0) == cap, tbl, x)
    send_ref[:, :d] = x.astype(BF16)
    send_ref[:, d:] = mm(perm, g_ref[...]).astype(BF16)


def forward(rows_x, w1, w3, w2):
    a = mm(rows_x, w1).astype(BF16).astype(F32)
    b = mm(rows_x, w3).astype(BF16).astype(F32)
    s = jax.nn.sigmoid(a)
    silu = a * s
    h = (silu * b).astype(BF16)
    out = mm(h, w2).astype(BF16)
    return a, b, s, silu, h, out


def backward(fwd, rows_g, w1, w3, w2):
    a, b, s, silu, h, out = fwd
    dh = mm_nt(rows_g, w2).astype(BF16).astype(F32)
    da = (dh * b * (s * (1.0 + a * (1.0 - s)))).astype(BF16)
    db = (dh * silu).astype(BF16)
    dx = (mm_nt(da, w1) + mm_nt(db, w3)).astype(BF16)
    return da, db, dx


def window(tbl_ref, src, expert, slab, rows_n):
    first = src * slab + tbl_ref[src, 64 + expert]
    count = tbl_ref[src, expert]
    base = pl.multiple_of(jnp.minimum((first // 16) * 16, rows_n - WIN), 16)
    return base, first - base, count


def inside(shape, off, count):
    r = iota(shape, 0)
    return (r >= off) & (r < off + count)


def load_rows(xg_ref, tbl_ref, expert, srcs, slab):
    parts = []
    for src in range(srcs):
        base, off, count = window(tbl_ref, src, expert, slab, xg_ref.shape[0])
        rows = xg_ref[pl.ds(base, WIN), :]
        parts.append(jnp.where(inside(rows.shape, off, count), rows, jnp.zeros_like(rows)))
    return jnp.concatenate(parts, axis=0)


def cold_kernel(srcs, slab, tbl_ref, xg_ref, w1_ref, w3_ref, w2_ref, od_ref, hab_ref):
    step = pl.program_id(0)
    expert = step + 1
    d = w1_ref.shape[1]

    @pl.when(step == 0)
    def _():
        od_ref[...] = jnp.zeros_like(od_ref)
        hab_ref[...] = jnp.zeros_like(hab_ref)

    rows = load_rows(xg_ref, tbl_ref, expert, srcs, slab)
    w1, w3, w2 = w1_ref[0], w3_ref[0], w2_ref[0]
    fwd = forward(rows[:, :d], w1, w3, w2)
    da, db, dx = backward(fwd, rows[:, d:], w1, w3, w2)
    od = jnp.concatenate([fwd[5], dx], axis=1)
    hab = jnp.concatenate([fwd[4], da, db], axis=1)
    for src in range(srcs):
        base, off, count = window(tbl_ref, src, expert, slab, xg_ref.shape[0])
        at = pl.ds(base, WIN)
        span = slice(src * WIN, (src + 1) * WIN)
        for ref, new in ((od_ref, od[span]), (hab_ref, hab[span])):
            ref[at, :] = jnp.where(inside(new.shape, off, count), new, ref[at, :])


def hot_kernel(xg_ref, w1_ref, w3_ref, w2_ref, od_ref, g1_ref, g3_ref, g2_ref):
    step = pl.program_id(0)
    d = w1_ref.shape[1]
    x, g = xg_ref[:, :d], xg_ref[:, d:]
    w1, w3, w2 = w1_ref[0], w3_ref[0], w2_ref[0]
    fwd = forward(x, w1, w3, w2)
    da, db, dx = backward(fwd, g, w1, w3, w2)
    od_ref[:, :d] = fwd[5]
    od_ref[:, d:] = dx

    @pl.when(step == 0)
    def _():
        for ref in (g1_ref, g3_ref, g2_ref):
            ref[...] = jnp.zeros_like(ref)

    g1_ref[...] += mm_tn(x, da)
    g3_ref[...] += mm_tn(x, db)
    g2_ref[...] += mm_tn(fwd[4], g)


def grad_kernel(srcs, slab, tbl_ref, xg_ref, hab_ref, h1_ref, h3_ref, h2_ref, g1_ref, g3_ref, g2_ref):
    expert = pl.program_id(0)
    d, f = h1_ref.shape

    @pl.when(expert == 0)
    def _():
        g1_ref[0] = h1_ref[...]
        g3_ref[0] = h3_ref[...]
        g2_ref[0] = h2_ref[...]

    @pl.when(expert > 0)
    def _():
        rows = load_rows(xg_ref, tbl_ref, expert, srcs, slab)
        hab = jnp.concatenate([hab_ref[pl.ds(window(tbl_ref, s, expert, slab, xg_ref.shape[0])[0], WIN), :] for s in range(srcs)], axis=0)
        x, g = rows[:, :d], rows[:, d:]
        g1_ref[0] = mm_tn(x, hab[:, f:2 * f])
        g3_ref[0] = mm_tn(x, hab[:, 2 * f:])
        g2_ref[0] = mm_tn(hab[:, :f], g)


def combine_kernel(first_list, cap, slab, round_ref, vslot_ref, gate_ref, ret_ref, *refs):
    y_ref, dx_ref = refs[-2:]
    d = y_ref.shape[1]
    vslot = to_column(vslot_ref[...].astype(F32))
    lane = iota((1, ret_ref.shape[0]), 1)
    dest = jnp.zeros_like(lane)
    for k in range(1, ret_ref.shape[0] // slab):
        dest += jnp.where(lane >= k * slab, 1, 0)
    row = lane - dest * slab
    have = jnp.where(row < cap, (dest + first_list) * LIST + round_ref[0] * cap + row, -2).astype(F32)
    pick = jnp.where(have == vslot, 1.0, 0.0).astype(BF16)
    y = (to_column(gate_ref[...]) * mm(pick, ret_ref[:, :d])).astype(BF16)
    dx = mm(pick, ret_ref[:, d:]).astype(BF16)
    if len(refs) == 4:
        y = y + refs[0][...]
        dx = dx + refs[1][...]
    y_ref[...] = y
    dx_ref[...] = dx


def params(mib):
    return pltpu.CompilerParams(vmem_limit_bytes=mib * 2 ** 20, dimension_semantics=('arbitrary',))


def cost(flops, nbytes):
    return pl.CostEstimate(flops=int(flops), bytes_accessed=int(nbytes), transcendentals=0)


def prefetched(grid, in_specs, out_specs, scratch=()):
    return pltpu.PrefetchScalarGridSpec(num_scalar_prefetch=1, grid=grid, in_specs=in_specs, out_specs=out_specs, scratch_shapes=list(scratch))


COLD_SLAB, COLD_CAP, HOT_SLAB = 272, 271, 288


def solution(mesh):
    srcs = mesh.shape['expert']
    tok_spec = P(('data', 'expert'))
    weight_spec = P('expert')
    whole = functools.partial(pl.BlockSpec, pipeline_mode=pl.Buffered(1))
    sds = jax.ShapeDtypeStruct
    fixed = lambda i, t: (0, 0)

    def shard_body(tok_x, route_idx, route_gate, grad_y, w_gate, w_up, w_down):
        tok_n, d = tok_x.shape
        local_n, _, f = w_gate.shape
        capacity = max(4, 2 * tok_n // (local_n * srcs))
        ids_row = route_idx.reshape(1, tok_n)
        gate_row = route_gate.reshape(1, tok_n)
        w_bytes = local_n * 3 * d * f * 2
        cold_rows, hot_rows = srcs * COLD_SLAB, srcs * HOT_SLAB

        vslot, tbl = pl.pallas_call(
            functools.partial(route_kernel, capacity, (COLD_CAP, HOT_SLAB)),
            out_shape=[sds((1, tok_n), I32), sds((8, 256), F32)],
            scratch_shapes=[pltpu.VMEM((1, tok_n), F32)],
            name='route',
        )(ids_row)

        def pack(rnd, first_list, cap, slab):
            return pl.pallas_call(
                functools.partial(pack_kernel, first_list, cap),
                grid_spec=prefetched(
                    (srcs,),
                    [whole((1, tok_n), fixed), whole((1, tok_n), fixed), whole((tok_n, d), fixed), whole((tok_n, d), fixed), whole((8, 256), fixed)],
                    pl.BlockSpec((slab, 2 * d), lambda i, t: (i, 0)),
                    [pltpu.VMEM((tok_n, d), BF16)],
                ),
                out_shape=sds((srcs * slab, 2 * d), BF16),
                compiler_params=params(48),
                cost_estimate=cost(2 * srcs * slab * tok_n * 2 * d, 2 * tok_n * d * 4),
                name='pack',
            )(rnd, vslot, gate_row, tok_x, grad_y, tbl)

        def exchange(rows, slab):
            return lax.all_to_all(rows.reshape(srcs, slab, 2 * d), 'expert', 0, 0).reshape(srcs * slab, 2 * d)

        def combine(rnd, first_list, cap, slab, ret, parts):
            blk = pl.BlockSpec((256, d), lambda i, t: (i, 0))
            row = pl.BlockSpec((1, 256), lambda i, t: (0, i))
            return pl.pallas_call(
                functools.partial(combine_kernel, first_list, cap, slab),
                grid_spec=prefetched((tok_n // 256,), [row, row, whole((srcs * slab, 2 * d), fixed)] + [blk] * len(parts), [blk, blk]),
                out_shape=[sds((tok_n, d), BF16), sds((tok_n, d), BF16)],
                compiler_params=params(48),
                cost_estimate=cost(2 * tok_n * srcs * slab * 2 * d, srcs * slab * 2 * d * 4),
                name='combine',
            )(rnd, vslot, gate_row, ret, *parts)

        def one_round(rnd):
            cold_xg = exchange(pack(rnd, 0, COLD_CAP, COLD_SLAB), COLD_SLAB)
            hot_xg = exchange(pack(rnd, srcs, HOT_SLAB, HOT_SLAB), HOT_SLAB)
            heads = cold_xg.reshape(srcs, COLD_SLAB, 2 * d)[:, COLD_CAP, :256].astype(I32)
            rel = heads[:, COL_HI:COL_HI + local_n] * 16 + heads[:, COL_LO:COL_LO + local_n] - rnd[0] * COLD_CAP
            end = jnp.clip(rel + heads[:, :local_n], 0, COLD_CAP)
            rel = jnp.clip(rel, 0, COLD_CAP)
            win_tbl = jnp.concatenate([end - rel, rel], axis=1)
            rounds = jnp.max(heads[:, COL_ROUNDS])

            cold_od, cold_hab = pl.pallas_call(
                functools.partial(cold_kernel, srcs, COLD_SLAB),
                grid_spec=prefetched(
                    (local_n - 1,),
                    [whole((cold_rows, 2 * d), fixed), pl.BlockSpec((1, d, f), lambda i, t: (i + 1, 0, 0)), pl.BlockSpec((1, d, f), lambda i, t: (i + 1, 0, 0)), pl.BlockSpec((1, f, d), lambda i, t: (i + 1, 0, 0))],
                    [whole((cold_rows, 2 * d), fixed), whole((cold_rows, 3 * f), fixed)],
                ),
                out_shape=[sds((cold_rows, 2 * d), BF16), sds((cold_rows, 3 * f), BF16)],
                compiler_params=params(48),
                cost_estimate=cost(2 * 6 * 512 * local_n * d * f, w_bytes),
                name='cold',
            )(win_tbl, cold_xg, w_gate, w_up, w_down)
            cold_ret = exchange(cold_od, COLD_SLAB)

            first = lambda i: (0, 0, 0)
            flat = lambda i: (0, 0)
            hot_blk = pl.BlockSpec((hot_rows // 2, 2 * d), lambda i: (i, 0))
            hot_od, hot1, hot3, hot2 = pl.pallas_call(
                hot_kernel,
                grid=(2,),
                in_specs=[hot_blk, whole((1, d, f), first), whole((1, d, f), first), whole((1, f, d), first)],
                out_specs=[hot_blk, whole((d, f), flat), whole((d, f), flat), whole((f, d), flat)],
                out_shape=[sds((hot_rows, 2 * d), BF16), sds((d, f), F32), sds((d, f), F32), sds((f, d), F32)],
                compiler_params=params(48),
                cost_estimate=cost(2 * 9 * hot_rows * d * f, 4 * hot_rows * d * 4),
                name='hot',
            )(hot_xg, w_gate, w_up, w_down)
            hot_ret = exchange(hot_od, HOT_SLAB)

            out3 = lambda i, t: (i, 0, 0)
            grads = pl.pallas_call(
                functools.partial(grad_kernel, srcs, COLD_SLAB),
                grid_spec=prefetched(
                    (local_n,),
                    [whole((cold_rows, 2 * d), fixed), whole((cold_rows, 3 * f), fixed), whole((d, f), fixed), whole((d, f), fixed), whole((f, d), fixed)],
                    [pl.BlockSpec((1, d, f), out3), pl.BlockSpec((1, d, f), out3), pl.BlockSpec((1, f, d), out3)],
                ),
                out_shape=[sds((local_n, d, f), F32), sds((local_n, d, f), F32), sds((local_n, f, d), F32)],
                compiler_params=params(48),
                cost_estimate=cost(2 * 3 * 512 * local_n * d * f, 2 * w_bytes),
                name='grads',
            )(win_tbl, cold_xg, cold_hab, hot1, hot3, hot2)

            parts = combine(rnd, 0, COLD_CAP, COLD_SLAB, cold_ret, ())
            y, dx = combine(rnd, srcs, HOT_SLAB, HOT_SLAB, hot_ret, parts)
            return rounds, (y, dx, *grads)

        rounds, outs = one_round(jnp.zeros((1,), I32))

        def more(state):
            return state[0][0] < rounds

        def again(state):
            _, extra = one_round(state[0])
            return (state[0] + 1, *(a + b for a, b in zip(state[1:], extra)))

        return lax.while_loop(more, again, (jnp.ones((1,), I32), *outs))[1:]

    return jax.shard_map(shard_body, mesh=mesh, in_specs=(tok_spec, tok_spec, tok_spec, tok_spec, weight_spec, weight_spec, weight_spec), out_specs=(tok_spec,) * 5, check_vma=False)
```

time: 602 us -> 283 us (0.47); the launches traced: 593 us -> 281 us
  matrix products: 222 us -> 0 us
  Pallas kernels: 0 us -> 195 us
  local copies, waits for them, and re-layouts: 193 us -> 7.4 us
  waiting for transfers between devices: 102 us -> 57.6 us
  other arithmetic: 34.9 us -> 0.83 us
  between operations: 15 us -> 0.88 us
  starting transfers between devices: 25.6 us -> 18.2 us
    dot_general x18 -> x0, matrix products: 222 us -> none  [the longest x2 31.2 us: expert_backward(): jnp.einsum(back_form, grad_b, w_lin, preferred_element_type=jnp.float32)]
    pallas_call x0 -> x8, Pallas kernels: none -> 195 us  [the longest x1 79.5 us: one_round(): pl.pallas_call(functools.partial(cold_kernel, srcs, COLD_SLAB), grid_spec...]
    gather x5 -> x0, local copies, waits for them, and re-layouts: 63.3 us -> none  [the longest x1 17.4 us: shard_body(): send_gate = gate_pad[slot_src].reshape(group_n, local_count, capacity)]
    reshape x8 -> x0, local copies, waits for them, and re-layouts: 47.1 us -> none  [the longest x2 15.1 us: shard_body(): send_dy = jnp.concatenate([grad_y, zero_row])[tok_src].reshape(buf_shape)]
    all_to_all x5 -> x4, waiting for transfers between devices: 102 us -> 57.6 us  [exchange(): lax.all_to_all(rows.reshape(srcs, slab, 2 * d), 'expert', 0, 0)]
    add x8 -> x0, local copies, waits for them, and re-layouts: 16.6 us -> none  [shard_body(): cold_w.at[local_list[slot_n]]]
    all_to_all x3 -> x0, local copies, waits for them, and re-layouts: 16.2 us -> none  [the longest x1 7.84 us: shard_body(): back_dx = lax.all_to_all(cold_dx, 'expert', 0, 0)]
    convert_element_type x2 -> x0, local copies, waits for them, and re-layouts: 15.2 us -> none  [the longest x1 7.66 us: expert_forward(): jnp.einsum(h_form + ',' + wo_form + '->' + out_form, hidden, w_out, prefe...]
  transfers between devices with their start and end apart: 7 -> 4, of which waited for: 3 -> 2; matrix products, arithmetic and copies ran while one was open for 67% -> 0% of each run, Pallas kernels for 0% -> 61%
where the time goes in v1:
time: 283 us; the launch traced here: 281 us
  Pallas kernels  195 us (69%)
  waiting for transfers between devices  57.6 us (20%)
  starting transfers between devices  18.2 us (6%)
  local copies, waits for them, and re-layouts  7.4 us (3%)
    pallas_call x1, Pallas kernels, one_round(): pl.pallas_call(functools.partial(cold_kernel, srcs, COLD_SLAB), grid_spec...  79.5 us
    pallas_call x1, Pallas kernels, one_round(): pl.pallas_call(functools.partial(grad_kernel, srcs, COLD_SLAB), grid_spec...  62.7 us
    all_to_all x4, waiting for transfers between devices, exchange(): lax.all_to_all(rows.reshape(srcs, slab, 2 * d), 'expert', 0, 0)  57.6 us
    pallas_call x2, Pallas kernels, combine(): pl.pallas_call(functools.partial(combine_kernel, first_list, cap, slab),...  21.5 us
    pallas_call x2, Pallas kernels, pack(): pl.pallas_call(functools.partial(pack_kernel, first_list, cap), grid_spec...  20.2 us
    all_to_all x4, starting transfers between devices, exchange(): lax.all_to_all(rows.reshape(srcs, slab, 2 * d), 'expert', 0, 0)  18.2 us
    pallas_call x1, Pallas kernels, one_round(): pl.pallas_call(hot_kernel, grid=(2,), in_specs=[hot_blk, whole((1, d, f),...  9.22 us
    unnamed x22, local copies, waits for them, and re-layouts  7.4 us
  transfers between devices with their start and end apart: 4, of which 2 were waited for; matrix products, arithmetic and copies ran while one was open for 0% of the time, Pallas kernels for 61%

profile of v1, /device:TPU:0, one launch (start us, length us, event | category | flops | bytes accessed | tf_op | source)
XLA Modules:
  0.0 280.8 jit_solution(11005831703142607247)
XLA Ops:
  0.6 2.4 route.1
  3.0 0.0 copy-start.16
  3.0 0.0 copy-start.21
  3.0 9.9 %pack.5 = bf16[1088,1536]{1,0:T(8,128)(2,1)} custom-call(s32[1]{0:T(128)} %constant.7.clone.1.round_ref, s32[1,1536]{1,0:T(1,128)S(1)} %get-tuple-element.268.vslot_ref, f32[1,1536]{1,0:T(1,128)} %bitcast.48, bf16[1536,768]{1,0:T(8,128)(2,1)} %x_ref.3, bf16[1536,768]{1,0:T(8,128)(2,1)} %dy_ref.3, f32[8,256]{1,0:T(8,128)S(1)} %get-tuple-element.272.tbl_ref), custom_call_target="tpu_custom_call" | custom-call | flops 5133828096 | bytes 9437184 | tf_op jit(solution)/shard_map/pack/pallas_call | solution.py:272
  13.0 0.0 copy-start.19
  13.0 4.7 %all-to-all-start.6 = ((bf16[4,272,1536]{2,1,0:T(8,128)(2,1)}), bf16[4,272,1536]{2,1,0:T(8,128)(2,1)S(1)}, u32[]{:S(2)}, u32[]{:S(2)}) async-start(bf16[4,272,1536]{2,1,0:T(8,128)(2,1)} %bitcast.18), calls=%async_computation.6 | async-start | bytes 6684672 | tf_op jit(solution)/shard_map/all_to_all | solution.py:287
  17.7 0.0 copy-done.16
  17.7 0.0 copy-done.21
  17.7 0.0 copy-done.19
  17.7 10.2 %pack.4 = bf16[1152,1536]{1,0:T(8,128)(2,1)} custom-call(s32[1]{0:T(128)} %constant.7.clone.1.round_ref, s32[1,1536]{1,0:T(1,128)S(1)} %get-tuple-element.268.vslot_ref, f32[1,1536]{1,0:T(1,128)S(1)} %bitcast.49, bf16[1536,768]{1,0:T(8,128)(2,1)} %x_ref.3, bf16[1536,768]{1,0:T(8,128)(2,1)} %dy_ref.3, f32[8,256]{1,0:T(8,128)S(1)} %get-tuple-element.272.tbl_ref), custom_call_target="tpu_custom_call" | custom-call | flops 5435817984 | bytes 9437184 | tf_op jit(solution)/shard_map/pack/pallas_call | solution.py:272
  28.0 28.7 %all-to-all-done.6 = bf16[4,272,1536]{2,1,0:T(8,128)(2,1)S(1)} async-done(((bf16[4,272,1536]{2,1,0:T(8,128)(2,1)}), bf16[4,272,1536]{2,1,0:T(8,128)(2,1)S(1)}, u32[]{:S(2)}, u32[]{:S(2)}) %all-to-all-start.6) | async-done | bytes 3342368 | tf_op jit(solution)/shard_map/all_to_all | solution.py:287
  56.7 0.0 copy-start.15
  56.7 0.1 fusion.5
  56.8 1.7 copy-done.15
  58.5 0.1 pad_add_fusion.1.tbl_ref
  58.5 3.7 %all-to-all-start.4 = ((bf16[4,288,1536]{2,1,0:T(8,128)(2,1)}), bf16[4,288,1536]{2,1,0:T(8,128)(2,1)S(1)}, u32[]{:S(2)}, u32[]{:S(2)}) async-start(bf16[4,288,1536]{2,1,0:T(8,128)(2,1)} %bitcast.14), calls=%async_computation.4 | async-start | bytes 7077888 | tf_op jit(solution)/shard_map/all_to_all | solution.py:287
  62.3 79.5 %cold.2 = (bf16[1088,1536]{1,0:T(8,128)(2,1)}, bf16[1088,768]{1,0:T(8,128)(2,1)S(1)}) custom-call(s32[4,128]{1,0:T(4,128)S(1)} %pad_add_fusion.1.tbl_ref, bf16[1088,1536]{1,0:T(8,128)(2,1)} %bitcast.45, bf16[64,768,256]{2,1,0:T(8,128)(2,1)} %w1_ref.3, bf16[64,768,256]{2,1,0:T(8,128)(2,1)} %w3_ref.3, bf16[64,256,768]{2,1,0:T(8,128)(2,1)} %w2_ref.3), custom_call_target="tpu_custom_call" | custom-call | flops 77309411328 | bytes 75497472 | tf_op jit(solution)/shard_map/cold/pallas_call | solution.py:311
  141.7 0.0 copy-start.4
  141.7 1.2 copy-done.4
  142.9 0.0 all-to-all-done.4
  142.9 0.0 copy-start.14
  142.9 4.8 %all-to-all-start.7 = ((bf16[4,272,1536]{2,1,0:T(8,128)(2,1)}), bf16[4,272,1536]{2,1,0:T(8,128)(2,1)}, u32[]{:S(2)}, u32[]{:S(2)}) async-start(bf16[4,272,1536]{2,1,0:T(8,128)(2,1)} %bitcast.22), calls=%async_computation.7 | async-start | bytes 6684672 | tf_op jit(solution)/shard_map/all_to_all | solution.py:287
  147.7 0.7 slice_reduce_fusion
  148.4 0.0 copy-done.14
  148.4 9.2 %hot.2 = (bf16[1152,1536]{1,0:T(8,128)(2,1)}, f32[768,256]{1,0:T(8,128)S(1)}, f32[768,256]{1,0:T(8,128)S(1)}, f32[256,768]{1,0:T(8,128)S(1)}) custom-call(bf16[1152,1536]{1,0:T(8,128)(2,1)} %bitcast.44, bf16[64,768,256]{2,1,0:T(8,128)(2,1)} %w1_ref.3, bf16[64,768,256]{2,1,0:T(8,128)(2,1)} %w3_ref.3, bf16[64,256,768]{2,1,0:T(8,128)(2,1)} %w2_ref.3), custom_call_target="tpu_custom_call" | custom-call | flops 4076863488 | bytes 14155776 | tf_op jit(solution)/shard_map/hot/pallas_call | solution.py:328
  157.6 28.8 %all-to-all-done.7 = bf16[4,272,1536]{2,1,0:T(8,128)(2,1)} async-done(((bf16[4,272,1536]{2,1,0:T(8,128)(2,1)}), bf16[4,272,1536]{2,1,0:T(8,128)(2,1)}, u32[]{:S(2)}, u32[]{:S(2)}) %all-to-all-start.7) | async-done | bytes 3342368 | tf_op jit(solution)/shard_map/all_to_all | solution.py:287
  186.4 4.9 %all-to-all-start.5 = ((bf16[4,288,1536]{2,1,0:T(8,128)(2,1)}), bf16[4,288,1536]{2,1,0:T(8,128)(2,1)}, u32[]{:S(2)}, u32[]{:S(2)}) async-start(bf16[4,288,1536]{2,1,0:T(8,128)(2,1)} %bitcast.16), calls=%async_computation.5 | async-start | bytes 7077888 | tf_op jit(solution)/shard_map/all_to_all | solution.py:287
  191.4 0.0 copy-start.5
  191.4 1.4 copy-done.5
  192.8 0.0 copy-start.22
  192.8 62.7 %grads.2 = (f32[64,768,256]{2,1,0:T(8,128)}, f32[64,768,256]{2,1,0:T(8,128)}, f32[64,256,768]{2,1,0:T(8,128)}) custom-call(s32[4,128]{1,0:T(4,128)S(1)} %pad_add_fusion.1.tbl_ref, bf16[1088,1536]{1,0:T(8,128)(2,1)} %bitcast.46, bf16[1088,768]{1,0:T(8,128)(2,1)S(1)} %copy-done.5, f32[768,256]{1,0:T(8,128)S(1)} %get-tuple-element.124.h1_ref, ...), custom_call_target="tpu_custom_call" | custom-call | flops 38654705664 | bytes 150994944 | tf_op jit(solution)/shard_map/grads/pallas_call | solution.py:341
  255.5 0.0 copy-done.22
  255.5 10.3 %combine.4 = (bf16[1536,768]{1,0:T(8,128)(2,1)S(1)}, bf16[1536,768]{1,0:T(8,128)(2,1)S(1)}) custom-call(s32[1]{0:T(128)} %constant.7.clone.1.round_ref, s32[1,1536]{1,0:T(1,128)S(1)} %copy-done.22, f32[1,1536]{1,0:T(1,128)S(1)} %bitcast.50, bf16[1088,1536]{1,0:T(8,128)(2,1)} %bitcast.23.ret_ref), custom_call_target="tpu_custom_call" | custom-call | flops 5133828096 | bytes 6684672 | tf_op jit(solution)/shard_map/combine/pallas_call | solution.py:292
  265.8 0.0 copy-start
  265.8 1.4 copy-done
  267.2 0.0 all-to-all-done.5
  267.2 0.0 copy-start.1
  267.2 1.7 copy-done.1
  268.9 0.0 copy-start.17
  268.9 11.2 %combine.5 = (bf16[1536,768]{1,0:T(8,128)(2,1)}, bf16[1536,768]{1,0:T(8,128)(2,1)}) custom-call(s32[1]{0:T(128)} %constant.7.clone.1.round_ref, s32[1,1536]{1,0:T(1,128)S(1)} %copy-done.22, f32[1,1536]{1,0:T(1,128)S(1)} %bitcast.51, bf16[1152,1536]{1,0:T(8,128)(2,1)} %bitcast.17.ret_ref, bf16[1536,768]{1,0:T(8,128)(2,1)S(1)} %get-tuple-element.119.refs_0_, ...), custom_call_target="tpu_custom_call" | custom-call | flops 5435817984 | bytes 7077888 | tf_op jit(solution)/shard_map/combine/pallas_call | solution.py:292
  280.1 0.0 copy-done.17
  280.1 0.6 while.18
  (2 shorter events, 0.0 us)
Async XLA Ops:
  3.0 14.7 %copy-start.16 = (f32[8,256]{1,0:T(8,128)}, f32[8,256]{1,0:T(8,128)S(1)}, u32[]{:S(2)}) copy-start(f32[8,256]{1,0:T(8,128)S(1)} %get-tuple-element.272.tbl_ref) | copy-start | bytes 24580
  3.0 14.7 %copy-start.21 = (s32[1,1536]{1,0:T(1,128)}, s32[1,1536]{1,0:T(1,128)S(1)}, u32[]{:S(2)}) copy-start(s32[1,1536]{1,0:T(1,128)S(1)} %get-tuple-element.268.vslot_ref) | copy-start | bytes 18436
  13.0 4.8 %copy-start.19 = (f32[1536,1]{0,1:T(1,128)S(1)}, f32[1536,1]{0,1:T(1,128)}, u32[]{:S(2)}) copy-start(f32[1536,1]{0,1:T(1,128)} %param.11) | copy-start | bytes 18436
  13.0 43.7 %all-to-all-start.6 = ((bf16[4,272,1536]{2,1,0:T(8,128)(2,1)}), bf16[4,272,1536]{2,1,0:T(8,128)(2,1)S(1)}, u32[]{:S(2)}, u32[]{:S(2)}) async-start(bf16[4,272,1536]{2,1,0:T(8,128)(2,1)} %bitcast.18), calls=%async_computation.6 | async-start | bytes 6684672 | tf_op jit(solution)/shard_map/all_to_all | solution.py:287
  56.7 1.8 copy-start.15
  58.5 84.4 %all-to-all-start.4 = ((bf16[4,288,1536]{2,1,0:T(8,128)(2,1)}), bf16[4,288,1536]{2,1,0:T(8,128)(2,1)S(1)}, u32[]{:S(2)}, u32[]{:S(2)}) async-start(bf16[4,288,1536]{2,1,0:T(8,128)(2,1)} %bitcast.14), calls=%async_computation.4 | async-start | bytes 7077888 | tf_op jit(solution)/shard_map/all_to_all | solution.py:287
  141.7 1.2 copy-start.4
  142.9 5.4 %copy-start.14 = (bf16[4,288,1536]{2,1,0:T(8,128)(2,1)}, bf16[4,288,1536]{2,1,0:T(8,128)(2,1)S(1)}, u32[]{:S(2)}) copy-start(bf16[4,288,1536]{2,1,0:T(8,128)(2,1)S(1)} %all-to-all-done.4) | copy-start | bytes 10616836
  142.9 43.5 %all-to-all-start.7 = ((bf16[4,272,1536]{2,1,0:T(8,128)(2,1)}), bf16[4,272,1536]{2,1,0:T(8,128)(2,1)}, u32[]{:S(2)}, u32[]{:S(2)}) async-start(bf16[4,272,1536]{2,1,0:T(8,128)(2,1)} %bitcast.22), calls=%async_computation.7 | async-start | bytes 6684672 | tf_op jit(solution)/shard_map/all_to_all | solution.py:287
  186.4 80.8 %all-to-all-start.5 = ((bf16[4,288,1536]{2,1,0:T(8,128)(2,1)}), bf16[4,288,1536]{2,1,0:T(8,128)(2,1)}, u32[]{:S(2)}, u32[]{:S(2)}) async-start(bf16[4,288,1536]{2,1,0:T(8,128)(2,1)} %bitcast.16), calls=%async_computation.5 | async-start | bytes 7077888 | tf_op jit(solution)/shard_map/all_to_all | solution.py:287
  191.4 1.4 copy-start.5
  192.8 62.7 %copy-start.22 = (s32[1,1536]{1,0:T(1,128)S(1)}, s32[1,1536]{1,0:T(1,128)}, u32[]{:S(2)}) copy-start(s32[1,1536]{1,0:T(1,128)} %copy-done.21) | copy-start | bytes 18436
  265.8 1.4 copy-start
  267.2 1.7 copy-start.1
  268.9 11.2 %copy-start.17 = (f32[8,256]{1,0:T(8,128)S(1)}, f32[8,256]{1,0:T(8,128)}, u32[]{:S(2)}) copy-start(f32[8,256]{1,0:T(8,128)} %copy-done.16) | copy-start | bytes 24580
